TPU v7x, 32 devices: a whole 2x2x4 slice. The times are simulated.
32 devices in a mesh: rep: 2 (over core), row: 16 (over z, y, x).
Axes of the slice: x: 2, y: 2, z: 4, core: 2. Of those that a mesh axis runs over, the one named last changes fastest.
Arguments:
- tiles: bfloat16 [128, 16, 128, 128], P('row', 'rep'), as said below
- tile_cols: int32 [128, 16], replicated, may hold values from -1 to 127, as said below
Outputs:
- vertex_counts: float32 [128, 128], P('row', 'rep')
Inputs may be any that keep to these rules, and one draw needn't show every extreme that they name: `tile_cols`: in each tile row I the filled slots come first and hold distinct tile columns from I - 32 to I, in increasing order; empty slots hold -1. At most 16 slots of a row are filled, and some row has all 16 filled. `tiles`: tiles of empty slots are zero; a tile on the diagonal (column equal to row) is zero on and above its own diagonal.
All inputs are finite; a program needn't handle non-finite values.
Results may differ from a plain program's by a relative error of at most 0.0003.
Values may be sent and summed in bfloat16 or wider, within the bound.
No kernel may reach another device: no remote copies, remote signals or barrier semaphores. Data moves between devices by JAX's collectives and lax.ppermute only.
A program may use at most 128 MiB of HBM per device.

v0:
```python
import jax
import jax.numpy as jnp
from jax import lax
from jax.sharding import PartitionSpec as P

BACK = 4


def from_partner(x, axis, distance):
    return lax.ppermute(x, axis, [(i, i ^ 1 << distance) for i in range(lax.axis_size(axis))])


def shifted(block, axis, distance):
    devices = range(lax.axis_size(axis))
    route = [(i - distance, i) for i in devices if i - distance in devices]
    return lax.ppermute(block, axis, route)


def row_counts(pool, tile_cols, base, slot_start, width):
    pool_rows = pool.shape[0]

    def one_row(item):
        whole_row, cols = item
        local = jnp.clip(cols - base, 0, pool_rows - 1)
        panels = jnp.take(pool, local, axis=0)
        safe = jnp.maximum(cols, 0)
        named = jnp.take(tile_cols, safe, axis=0)
        panel_cols = lax.dynamic_slice_in_dim(named, slot_start, width, 1)
        match = (panel_cols[:, :, None] == cols[None, None, :]) & (cols >= 0)[None, None, :]
        masks = jnp.einsum(
            "kjp,pac->kjac",
            match.astype(jnp.bfloat16),
            whole_row,
            preferred_element_type=jnp.float32,
        ).astype(jnp.bfloat16)
        product = jnp.einsum(
            "kab,kjbc->kjac", whole_row, panels, preferred_element_type=jnp.float32
        )
        return jnp.sum(product * masks.astype(jnp.float32), axis=(0, 1, 3))

    return one_row


def body(tiles, tile_cols):
    rows_here, half_slots, tile, _ = tiles.shape
    index_rep = lax.axis_index("rep")
    index_row = lax.axis_index("row")
    partner = from_partner(tiles, "rep", 0)
    first = jnp.where(index_rep == 0, tiles, partner)
    second = jnp.where(index_rep == 0, partner, tiles)
    full = jnp.concatenate([first, second], axis=1)
    my_cols = lax.dynamic_slice_in_dim(tile_cols, index_row * rows_here, rows_here, 0)
    base = (index_row - BACK) * rows_here
    earlier = [shifted(tiles, "row", BACK - step) for step in range(BACK)]
    pool = jnp.concatenate(earlier + [tiles], axis=0)
    one_row = row_counts(pool, tile_cols, base, index_rep * half_slots, half_slots)
    partial_counts = lax.map(one_row, (full, my_cols))
    counts = lax.psum_scatter(partial_counts, "rep", scatter_dimension=1, tiled=True)
    return counts


def solution(mesh):
    return jax.shard_map(
        body,
        mesh=mesh,
        in_specs=(P("row", "rep", None, None), P()),
        out_specs=P("row", "rep"),
        check_vma=False,
    )
```

profile of v0, /device:TPU:25, one launch (start us, length us, event | category | flops | bytes accessed | tf_op | source)
XLA Modules:
  0.0 419.2 jit_solution(4239679745414784118)
XLA Ops:
  17.6 37.6 %collective-permute-done = bf16[8,8,128,128]{3,2,1,0:T(8,128)(2,1)} collective-permute-done((bf16[8,8,128,128]{3,2,1,0:T(8,128)(2,1)}, bf16[8,8,128,128]{3,2,1,0:T(8,128)(2,1)}, u32[]{:S(2)}, u32[]{:S(2)}) %collective-permute-start) | collective-permute-done | bytes 2097184 | tf_op jit(solution)/shard_map/ppermute | solution.py:16
  58.4 42.7 %collective-permute-done.1 = bf16[8,8,128,128]{3,2,1,0:T(8,128)(2,1)} collective-permute-done((bf16[8,8,128,128]{3,2,1,0:T(8,128)(2,1)}, bf16[8,8,128,128]{3,2,1,0:T(8,128)(2,1)}, u32[]{:S(2)}, u32[]{:S(2)}) %collective-permute-start.1) | collective-permute-done | bytes 2097184 | tf_op jit(solution)/shard_map/ppermute | solution.py:16
  104.3 41.8 %collective-permute-done.2 = bf16[8,8,128,128]{3,2,1,0:T(8,128)(2,1)} collective-permute-done((bf16[8,8,128,128]{3,2,1,0:T(8,128)(2,1)}, bf16[8,8,128,128]{3,2,1,0:T(8,128)(2,1)}, u32[]{:S(2)}, u32[]{:S(2)}) %collective-permute-start.2) | collective-permute-done | bytes 2097184 | tf_op jit(solution)/shard_map/ppermute | solution.py:16
  149.3 42.6 %collective-permute-done.3 = bf16[8,8,128,128]{3,2,1,0:T(8,128)(2,1)S(1)} collective-permute-done((bf16[8,8,128,128]{3,2,1,0:T(8,128)(2,1)}, bf16[8,8,128,128]{3,2,1,0:T(8,128)(2,1)S(1)}, u32[]{:S(2)}, u32[]{:S(2)}) %collective-permute-start.3) | collective-permute-done | bytes 2097184 | tf_op jit(solution)/shard_map/ppermute | solution.py:16
  200.2 201.6 %while.12 = (s32[]{:T(128)}, f32[8,128]{1,0:T(8,128)S(1)}, s32[8,16]{1,0:T(8,128)S(1)}, s32[]{:T(128)}, bf16[40,8,128,128]{3,2,1,0:T(8,128)(2,1)}, /*index=5*/bf...) while((s32[]{:T(128)}, f32[8,128]{1,0:T(8,128)S(1)}, ...), condition=%wide.region_2.3_spmd, body=%wide.region_0.2_spmd.sunk | while | flops 612374784 | bytes 31472092 | solution.py:57
  205.3 6.8 %copy.25 = bf16[16,8,128,128]{2,3,1,0:T(8,128)(2,1)} copy(bf16[16,8,128,128]{3,1,2,0:T(8,128)(2,1)} %fusion.32) | data formatting | bytes 8388608 | tf_op jit(solution)/shard_map/while/body/eval_jaxpr/kjp,pac->kjac/dot_general | solution.py:30
  212.1 7.1 %gather_fusion.1 = bf16[16,8,128,128]{3,2,1,0:T(8,128)(2,1)} fusion(bf16[40,8,128,128]{3,2,1,0:T(8,128)(2,1)} %get-tuple-element.222, s32[1024]{0:T(1024)S(1)} %pad_clamp_fusion.5), kind=kCustom, calls=%fused_computation.clone.1 | custom fusion | bytes 8388672 | tf_op jit(solution)/shard_map/while/body/eval_jaxpr/jit(_take)/gather | solution.py:25
  219.2 6.2 %fusion.34 = f32[128]{0:T(128)S(1)} fusion(bf16[16,8,128,128]{2,3,1,0:T(8,128)(2,1)} %copy.25, bf16[16,8,128,128]{3,2,1,0:T(8,128)(2,1)} %gather_fusion.1, pred[16]{0:T(512)(128)(4,1)S(1)} %get-tuple-element.197, bf16[8,16,128,128]{3,2,1,0:T(8,128)(2,1)} %get-tuple-element.223, s32[]{:T(128)} %get-tuple-element.208), kind=kOutput, calls=%fused_computation.3.clone.1 | convolution fusion | flops 545259392 | bytes 8913936 | tf_op jit(solution)/shard_map/while/body/eval_jaxpr/kab,kjbc->kjac/dot_general | solution.py:36
  230.5 6.8 %copy.25 = bf16[16,8,128,128]{2,3,1,0:T(8,128)(2,1)} copy(bf16[16,8,128,128]{3,1,2,0:T(8,128)(2,1)} %fusion.32) | data formatting | bytes 8388608 | tf_op jit(solution)/shard_map/while/body/eval_jaxpr/kjp,pac->kjac/dot_general | solution.py:30
  237.3 7.1 %gather_fusion.1 = bf16[16,8,128,128]{3,2,1,0:T(8,128)(2,1)} fusion(bf16[40,8,128,128]{3,2,1,0:T(8,128)(2,1)} %get-tuple-element.222, s32[1024]{0:T(1024)S(1)} %pad_clamp_fusion.5), kind=kCustom, calls=%fused_computation.clone.1 | custom fusion | bytes 8388672 | tf_op jit(solution)/shard_map/while/body/eval_jaxpr/jit(_take)/gather | solution.py:25
  244.4 6.2 %fusion.34 = f32[128]{0:T(128)S(1)} fusion(bf16[16,8,128,128]{2,3,1,0:T(8,128)(2,1)} %copy.25, bf16[16,8,128,128]{3,2,1,0:T(8,128)(2,1)} %gather_fusion.1, pred[16]{0:T(512)(128)(4,1)S(1)} %get-tuple-element.197, bf16[8,16,128,128]{3,2,1,0:T(8,128)(2,1)} %get-tuple-element.223, s32[]{:T(128)} %get-tuple-element.208), kind=kOutput, calls=%fused_computation.3.clone.1 | convolution fusion | flops 545259392 | bytes 8913936 | tf_op jit(solution)/shard_map/while/body/eval_jaxpr/kab,kjbc->kjac/dot_general | solution.py:36
  255.7 6.8 %copy.25 = bf16[16,8,128,128]{2,3,1,0:T(8,128)(2,1)} copy(bf16[16,8,128,128]{3,1,2,0:T(8,128)(2,1)} %fusion.32) | data formatting | bytes 8388608 | tf_op jit(solution)/shard_map/while/body/eval_jaxpr/kjp,pac->kjac/dot_general | solution.py:30
  262.5 7.1 %gather_fusion.1 = bf16[16,8,128,128]{3,2,1,0:T(8,128)(2,1)} fusion(bf16[40,8,128,128]{3,2,1,0:T(8,128)(2,1)} %get-tuple-element.222, s32[1024]{0:T(1024)S(1)} %pad_clamp_fusion.5), kind=kCustom, calls=%fused_computation.clone.1 | custom fusion | bytes 8388672 | tf_op jit(solution)/shard_map/while/body/eval_jaxpr/jit(_take)/gather | solution.py:25
  280.9 6.8 %copy.25 = bf16[16,8,128,128]{2,3,1,0:T(8,128)(2,1)} copy(bf16[16,8,128,128]{3,1,2,0:T(8,128)(2,1)} %fusion.32) | data formatting | bytes 8388608 | tf_op jit(solution)/shard_map/while/body/eval_jaxpr/kjp,pac->kjac/dot_general | solution.py:30
  287.7 7.1 %gather_fusion.1 = bf16[16,8,128,128]{3,2,1,0:T(8,128)(2,1)} fusion(bf16[40,8,128,128]{3,2,1,0:T(8,128)(2,1)} %get-tuple-element.222, s32[1024]{0:T(1024)S(1)} %pad_clamp_fusion.5), kind=kCustom, calls=%fused_computation.clone.1 | custom fusion | bytes 8388672 | tf_op jit(solution)/shard_map/while/body/eval_jaxpr/jit(_take)/gather | solution.py:25
  306.1 6.8 %copy.25 = bf16[16,8,128,128]{2,3,1,0:T(8,128)(2,1)} copy(bf16[16,8,128,128]{3,1,2,0:T(8,128)(2,1)} %fusion.32) | data formatting | bytes 8388608 | tf_op jit(solution)/shard_map/while/body/eval_jaxpr/kjp,pac->kjac/dot_general | solution.py:30
  312.9 7.1 %gather_fusion.1 = bf16[16,8,128,128]{3,2,1,0:T(8,128)(2,1)} fusion(bf16[40,8,128,128]{3,2,1,0:T(8,128)(2,1)} %get-tuple-element.222, s32[1024]{0:T(1024)S(1)} %pad_clamp_fusion.5), kind=kCustom, calls=%fused_computation.clone.1 | custom fusion | bytes 8388672 | tf_op jit(solution)/shard_map/while/body/eval_jaxpr/jit(_take)/gather | solution.py:25
  331.4 6.8 %copy.25 = bf16[16,8,128,128]{2,3,1,0:T(8,128)(2,1)} copy(bf16[16,8,128,128]{3,1,2,0:T(8,128)(2,1)} %fusion.32) | data formatting | bytes 8388608 | tf_op jit(solution)/shard_map/while/body/eval_jaxpr/kjp,pac->kjac/dot_general | solution.py:30
  338.2 7.1 %gather_fusion.1 = bf16[16,8,128,128]{3,2,1,0:T(8,128)(2,1)} fusion(bf16[40,8,128,128]{3,2,1,0:T(8,128)(2,1)} %get-tuple-element.222, s32[1024]{0:T(1024)S(1)} %pad_clamp_fusion.5), kind=kCustom, calls=%fused_computation.clone.1 | custom fusion | bytes 8388672 | tf_op jit(solution)/shard_map/while/body/eval_jaxpr/jit(_take)/gather | solution.py:25
  356.6 6.8 %copy.25 = bf16[16,8,128,128]{2,3,1,0:T(8,128)(2,1)} copy(bf16[16,8,128,128]{3,1,2,0:T(8,128)(2,1)} %fusion.32) | data formatting | bytes 8388608 | tf_op jit(solution)/shard_map/while/body/eval_jaxpr/kjp,pac->kjac/dot_general | solution.py:30
  363.4 7.1 %gather_fusion.1 = bf16[16,8,128,128]{3,2,1,0:T(8,128)(2,1)} fusion(bf16[40,8,128,128]{3,2,1,0:T(8,128)(2,1)} %get-tuple-element.222, s32[1024]{0:T(1024)S(1)} %pad_clamp_fusion.5), kind=kCustom, calls=%fused_computation.clone.1 | custom fusion | bytes 8388672 | tf_op jit(solution)/shard_map/while/body/eval_jaxpr/jit(_take)/gather | solution.py:25
  381.8 6.8 %copy.25 = bf16[16,8,128,128]{2,3,1,0:T(8,128)(2,1)} copy(bf16[16,8,128,128]{3,1,2,0:T(8,128)(2,1)} %fusion.32) | data formatting | bytes 8388608 | tf_op jit(solution)/shard_map/while/body/eval_jaxpr/kjp,pac->kjac/dot_general | solution.py:30
  388.6 7.1 %gather_fusion.1 = bf16[16,8,128,128]{3,2,1,0:T(8,128)(2,1)} fusion(bf16[40,8,128,128]{3,2,1,0:T(8,128)(2,1)} %get-tuple-element.222, s32[1024]{0:T(1024)S(1)} %pad_clamp_fusion.5), kind=kCustom, calls=%fused_computation.clone.1 | custom fusion | bytes 8388672 | tf_op jit(solution)/shard_map/while/body/eval_jaxpr/jit(_take)/gather | solution.py:25
  402.6 8.4 %reduce-scatter.4.cloned.1.call-done = f32[64,8]{1,0:T(8,128)} async-done(((f32[128,8]{1,0:T(8,128)}), f32[64,8]{1,0:T(8,128)}) %reduce-scatter.4.cloned.1.call-update) | async-done | bytes 2064
  (115 shorter events, 109.0 us)
Async XLA Ops:
  6.5 404.4 %reduce-scatter.4.cloned.1.call-start = ((), (), s32[]{:S(2)}) async-start(), calls=%async_computation.1 | async-start | bytes 98304
  6.5 48.7 %collective-permute-start = (bf16[8,8,128,128]{3,2,1,0:T(8,128)(2,1)}, bf16[8,8,128,128]{3,2,1,0:T(8,128)(2,1)}, u32[]{:S(2)}, u32[]{:S(2)}) collective-permute-start(bf16[8,8,128,128]{3,2,1,0:T(8,128)(2,1)} %param.4), channel_id=1, source_target_pairs={{0,4},{1,5},{2,6},{3,7},{4,8},{5,9},{6,10},{7,11},{8,12},{9,13},{1... | collective-permute-start | bytes 6291464 | tf_op jit(solution)/shard_map/ppermute | solution.py:16
  7.8 93.3 %collective-permute-start.1 = (bf16[8,8,128,128]{3,2,1,0:T(8,128)(2,1)}, bf16[8,8,128,128]{3,2,1,0:T(8,128)(2,1)}, u32[]{:S(2)}, u32[]{:S(2)}) collective-permute-start(bf16[8,8,128,128]{3,2,1,0:T(8,128)(2,1)} %param.4), channel_id=1, source_target_pairs={{0,3},{1,4},{2,5},{3,6},{4,7},{5,8},{6,9},{7,10},{8,11},{9,12},{10... | collective-permute-start | bytes 6291464 | tf_op jit(solution)/shard_map/ppermute | solution.py:16
  11.9 134.2 %collective-permute-start.2 = (bf16[8,8,128,128]{3,2,1,0:T(8,128)(2,1)}, bf16[8,8,128,128]{3,2,1,0:T(8,128)(2,1)}, u32[]{:S(2)}, u32[]{:S(2)}) collective-permute-start(bf16[8,8,128,128]{3,2,1,0:T(8,128)(2,1)} %param.4), channel_id=1, source_target_pairs={{0,2},{1,3},{2,4},{3,5},{4,6},{5,7},{6,8},{7,9},{8,10},{9,11},{10,... | collective-permute-start | bytes 6291464 | tf_op jit(solution)/shard_map/ppermute | solution.py:16
  13.8 178.0 %collective-permute-start.3 = (bf16[8,8,128,128]{3,2,1,0:T(8,128)(2,1)}, bf16[8,8,128,128]{3,2,1,0:T(8,128)(2,1)S(1)}, u32[]{:S(2)}, u32[]{:S(2)}) collective-permute-start(bf16[8,8,128,128]{3,2,1,0:T(8,128)(2,1)} %param.4), channel_id=1, source_target_pairs={{0,1},{1,2},{2,3},{3,4},{4,5},{5,6},{6,7},{7,8},{8,9},{9,10},{10,1... | collective-permute-start | bytes 6291464 | tf_op jit(solution)/shard_map/ppermute | solution.py:16
  15.8 177.6 %collective-permute-start.4 = (bf16[8,8,128,128]{3,2,1,0:T(8,128)(2,1)}, bf16[8,8,128,128]{3,2,1,0:T(8,128)(2,1)}, u32[]{:S(2)}, u32[]{:S(2)}) collective-permute-start(bf16[8,8,128,128]{3,2,1,0:T(8,128)(2,1)} %param.4), channel_id=1, source_target_pairs={{0,16},{16,0},{1,17},{17,1},{2,18},{18,2},{3,19},{19,3},{4,20},{20... | collective-permute-start | bytes 6291464 | tf_op jit(solution)/shard_map/ppermute | solution.py:10
  104.3 89.1 %copy-start = (bf16[8,8,128,128]{3,2,1,0:T(8,128)(2,1)S(1)}, bf16[8,8,128,128]{3,2,1,0:T(8,128)(2,1)}, u32[]{:S(2)}) copy-start(bf16[8,8,128,128]{3,2,1,0:T(8,128)(2,1)} %param.4) | copy-start | bytes 6291460
Sparse Core Ops, SparseCore 0:
  402.7 8.1 reduce-scatter.3
where the time goes:
time: 422 us; the launch traced here: 419 us
  waiting for transfers between devices  173 us (41%)
  local copies, waits for them, and re-layouts  138 us (33%)
  matrix products  75.9 us (18%)
  between operations  13.4 us (3%)
  starting transfers between devices  10.2 us (2%)
  other arithmetic  7.87 us (2%)
    ppermute x4, waiting for transfers between devices, shifted(): return lax.ppermute(block, axis, route)  165 us
    gather x8, local copies, waits for them, and re-layouts, one_row(): panels = jnp.take(pool, local, axis=0)  56.7 us
    dot_general x8, local copies, waits for them, and re-layouts, one_row(): jnp.einsum('kjp,pac->kjac', match.astype(jnp.bfloat16), whole_row, prefer...  54.2 us
    dot_general x8, matrix products, one_row(): jnp.einsum('kab,kjbc->kjac', whole_row, panels, preferred_element_type=jn...  49.3 us
    dot_general x8, matrix products, one_row(): jnp.einsum('kjp,pac->kjac', match.astype(jnp.bfloat16), whole_row, prefer...  26.6 us
    unnamed x9, local copies, waits for them, and re-layouts  13.9 us
    ppermute x4, starting transfers between devices, shifted(): return lax.ppermute(block, axis, route)  9.2 us
    squeeze x8, local copies, waits for them, and re-layouts, body(): partial_counts = lax.map(one_row, (full, my_cols))  8.62 us
  transfers between devices with their start and end apart: 6, of which 5 were waited for; matrix products, arithmetic and copies ran while one was open for 3% of the time, Pallas kernels for 0%

commit v1 on v0

v1 whole, which is shorter than its diff:
```python
import jax
import jax.numpy as jnp
from jax import lax
from jax.experimental import pallas as pl
from jax.experimental.pallas import tpu as pltpu
from jax.sharding import PartitionSpec as P

BACK = 4
UNROLL = 8
OWN, SIDE, NEXT, UP3, UP, SIDE_NEXT, SIDE_UP, NEXT_UP, UP3_DIAG, UP_DOWN = range(10)
GROUPS = 10
ARRIVES = (
    (UP3_DIAG, NEXT_UP, UP_DOWN, UP),
    (SIDE, NEXT_UP, UP_DOWN, UP),
    (SIDE_NEXT, NEXT, SIDE_UP, UP),
    (SIDE, NEXT, SIDE_NEXT, UP3),
)


def swap_cores(x):
    return lax.ppermute(x, "rep", [(0, 1), (1, 0)])


def moved(x, steps):
    size = lax.axis_size("row")
    route = [(i, i + steps[i % BACK]) for i in range(size) if i % BACK in steps]
    return lax.ppermute(x, "row", [(i, j) for i, j in route if j < size])


def running(flags):
    n = flags.shape[-1]
    tri = (jnp.arange(n)[:, None] < jnp.arange(n)[None, :]).astype(jnp.bfloat16)
    flat = flags.reshape(-1, n).astype(jnp.bfloat16)
    count = jnp.dot(flat, tri, preferred_element_type=jnp.float32)
    return count.astype(jnp.int32).reshape(flags.shape)


def send_lists(tile_cols, rows):
    count, slots = tile_cols.shape
    blocks = count // rows
    every = jnp.arange(count, dtype=jnp.int32)
    hot = tile_cols[:, :, None] == every
    member = jnp.any(hot, axis=1).astype(jnp.bfloat16).reshape(blocks, rows, count)
    padded = jnp.pad(member, ((0, BACK), (0, 0), (0, 0)))
    later = jnp.concatenate([padded[d : d + blocks] for d in range(1, BACK + 1)], axis=1)
    column = hot.reshape(blocks, rows * slots, count).astype(jnp.bfloat16)
    line = jnp.broadcast_to((every[:, None] == every)[:, None, :], hot.shape)
    line = line.reshape(blocks, rows * slots, count).astype(jnp.bfloat16)
    dims = (((2,), (2,)), ((0,), (0,)))
    has_column = lax.dot_general(later, column, dims, preferred_element_type=jnp.float32)
    has_line = lax.dot_general(later, line, dims, preferred_element_type=jnp.float32)
    both = (has_column * has_line).reshape(blocks, BACK, rows, rows * slots)
    need = jnp.max(both, axis=2) > 0
    place = (jnp.arange(blocks) % BACK)[:, None]
    near, second, third, fourth = (need[:, d] for d in range(BACK))
    side = (near & (place != 3)) | (third & ((place == 0) | (place == 3)))
    upper = fourth | (near & (place == 3)) | (third & ((place == 1) | (place == 2)))
    return jnp.stack([side, second, upper], axis=1)


def gather_kernel(caps, lists, index_ref, mine_ref, other_ref, *rest):
    outs, pool, sem = rest[:-2], rest[-2], rest[-1]
    half = mine_ref.shape[0]
    first = pltpu.make_async_copy(mine_ref, pool.at[pl.ds(0, half)], sem.at[0])
    second = pltpu.make_async_copy(other_ref, pool.at[pl.ds(half, half)], sem.at[1])
    first.start()
    second.start()
    first.wait()
    second.wait()
    for out, cap, which in zip(outs, caps, lists):

        def one(p, carry, out=out, which=which):
            out[p] = pool[index_ref[which, p]]
            return carry

        lax.fori_loop(0, cap, one, 0, unroll=2)


def gather_tiles(caps, lists, index, mine, other):
    tile = mine.shape[-2:]
    anywhere = pl.BlockSpec(memory_space=pl.ANY)
    return pl.pallas_call(
        lambda *refs: gather_kernel(caps, lists, *refs),
        out_shape=[jax.ShapeDtypeStruct((cap,) + tile, mine.dtype) for cap in caps],
        in_specs=[pl.BlockSpec(memory_space=pltpu.SMEM), anywhere, anywhere],
        out_specs=[pl.BlockSpec(memory_space=pltpu.VMEM)] * len(caps),
        scratch_shapes=[
            pltpu.VMEM((2 * mine.shape[0],) + tile, mine.dtype),
            pltpu.SemaphoreType.DMA((2,)),
        ],
        cost_estimate=pl.CostEstimate(
            flops=10**6, bytes_accessed=sum(caps) * 65536, transcendentals=0
        ),
    )(index, mine, other)


def count_kernel(groups, rows, start_ref, item_ref, before_ref, mine_ref, other_ref, *rest):
    n = len(groups)
    bufs, out_ref, own, acc = rest[:n], rest[n], rest[n + 1], rest[n + 2]
    held, sem, own_sem = rest[n + 3 : 2 * n + 3], rest[-2], rest[-1]
    half = mine_ref.shape[0]
    slots_here = half // rows
    first = pltpu.make_async_copy(mine_ref, own.at[pl.ds(0, half)], own_sem.at[0])
    second = pltpu.make_async_copy(other_ref, own.at[pl.ds(half, half)], own_sem.at[1])
    first.start()
    second.start()
    for i, group in enumerate(groups):

        @pl.when(start_ref[group + 1] > start_ref[group])
        def _(i=i):
            pltpu.make_async_copy(bufs[i], held[i], sem.at[i]).start()

    own[2 * half] = jnp.zeros(own.shape[1:], own.dtype)
    acc[...] = jnp.zeros_like(acc)
    first.wait()
    second.wait()

    def work(group, source):
        def step(i, carry):
            for u in range(UNROLL):
                code = item_ref[i * UNROLL + u]
                a = code & 255
                b = (code >> 8) & 255
                t = code >> 16
                row = (a & (half - 1)) // slots_here
                product = jnp.dot(own[a], source[t], preferred_element_type=jnp.float32)
                acc[row] += product * own[b].astype(jnp.float32)
            return carry

        lax.fori_loop(start_ref[group], start_ref[group + 1], step, 0)

    if not groups:
        work(OWN, own)
    for i, group in enumerate(groups):

        @pl.when(start_ref[group + 1] > start_ref[group])
        def _(i=i, group=group):
            pltpu.make_async_copy(bufs[i], held[i], sem.at[i]).wait()
            work(group, held[i])

    out_ref[...] = before_ref[...] + jnp.sum(acc[...], axis=2)


def count_tiles(groups, rows, starts, items, before, mine, other, bufs, flops):
    half, tile, _ = mine.shape
    anywhere = pl.BlockSpec(memory_space=pl.ANY)
    vmem = pl.BlockSpec(memory_space=pltpu.VMEM)
    return pl.pallas_call(
        lambda *refs: count_kernel(groups, rows, *refs),
        out_shape=jax.ShapeDtypeStruct((rows, tile), jnp.float32),
        in_specs=[pl.BlockSpec(memory_space=pltpu.SMEM)] * 2 + [vmem] + [anywhere] * (2 + len(bufs)),
        out_specs=vmem,
        scratch_shapes=[
            pltpu.VMEM((2 * half + 1, tile, tile), mine.dtype),
            pltpu.VMEM((rows, tile, tile), jnp.float32),
        ]
        + [pltpu.VMEM(b.shape, b.dtype) for b in bufs]
        + [pltpu.SemaphoreType.DMA((max(1, len(bufs)),)), pltpu.SemaphoreType.DMA((2,))],
        cost_estimate=pl.CostEstimate(flops=flops, bytes_accessed=8 * 10**6, transcendentals=0),
    )(starts, items, before, mine, other, *bufs)


def work_items(tile_cols, lists, ranks, rows, half_slots, here, core, loc):
    count, slots = tile_cols.shape
    per_block = rows * slots
    half = rows * half_slots
    place = here % BACK
    window = (BACK + 1) * rows

    pad = ((BACK, 0), (0, 0), (0, 0))
    near_lists = lax.dynamic_slice_in_dim(jnp.pad(lists, pad), here, BACK, 0)
    near_ranks = lax.dynamic_slice_in_dim(jnp.pad(ranks, pad), here, BACK, 0)
    from_place = (here + jnp.arange(BACK)) % BACK
    dist = BACK - jnp.arange(BACK)
    upper = (dist == 4) | ((dist == 1) & (from_place == 3))
    upper = upper | ((dist == 3) & ((from_place == 1) | (from_place == 2)))
    which = jnp.where(dist == 2, 1, jnp.where(upper, 2, 0))
    pick = (which[:, None] == jnp.arange(3))[:, :, None]
    flag = jnp.any(near_lists & pick, axis=1)
    rank = jnp.sum(jnp.where(pick, near_ranks, 0), axis=1)
    spot = jnp.where(flag & (rank % 2 == core), rank // 2 + 1, 0)
    order = jnp.arange(per_block, dtype=jnp.int32)
    own_spot = jnp.where(order % 2 == core, loc + 1, 0)
    spot = jnp.concatenate([spot, own_spot[None]], axis=0)

    base = (here - BACK) * rows
    inside = jnp.arange(window, dtype=jnp.int32)
    padded = jnp.pad(tile_cols, ((BACK * rows, 0), (0, 0)), constant_values=-1)
    near = lax.dynamic_slice(padded, (here * rows, 0), (window, slots))
    hot = (near[:, :, None] - base == inside) & (near >= 0)[:, :, None]
    table = spot.reshape(window, slots)
    table = jnp.sum(jnp.where(hot, table[:, :, None], 0), axis=1).astype(jnp.bfloat16)
    mine_hot = hot[BACK * rows :].astype(jnp.bfloat16)
    found = jnp.einsum("ipk,kj->ipj", mine_hot, table, preferred_element_type=jnp.float32)
    found = jnp.einsum(
        "ipj,iqj->ipq", found.astype(jnp.bfloat16), mine_hot, preferred_element_type=jnp.float32
    ).astype(jnp.int32)
    my_cols = near[BACK * rows :]
    back = here - my_cols // rows
    group = jnp.zeros_like(back)
    for row in range(BACK):
        for d in range(1, BACK + 1):
            group = jnp.where((place == row) & (back == d), ARRIVES[row][d - 1], group)
    own_loc = loc.reshape(rows, slots)
    code = own_loc[:, :, None] + own_loc[:, None, :] * 256 + (found - 1) * 65536
    total = rows * slots * slots
    valid = (found > 0).reshape(total // 128, 128)
    group = jnp.broadcast_to(group[:, :, None], (rows, slots, slots)).reshape(total // 128, 128)
    ids = jnp.arange(GROUPS, dtype=jnp.int32)
    chosen = (group == ids[:, None, None]) & valid
    lane_rank = running(chosen)
    lane_sum = jnp.sum(chosen.astype(jnp.int32), axis=2)
    major = running(lane_sum)
    trips = (jnp.sum(lane_sum, axis=1) + UNROLL - 1) // UNROLL
    starts = jnp.sum(jnp.where(jnp.arange(GROUPS + 1)[:, None] > ids, trips, 0), axis=1)
    spread = lane_rank + (major + starts[:GROUPS, None] * UNROLL + 1)[:, :, None]
    target = jnp.sum(jnp.where(chosen, spread, 0), axis=0).reshape(1, total)
    dummy = 256 * 2 * half
    limit = rows * slots * (slots + 1) // 2 + GROUPS * UNROLL
    limit = -(-limit // 128) * 128
    at = jnp.arange(1, limit + 1, dtype=jnp.int32)[:, None]
    hit = jnp.where(target == at, code.reshape(1, total) - dummy, 0)
    return starts, dummy + jnp.sum(hit, axis=1)


def body(tiles, tile_cols):
    rows, half_slots, tile, _ = tiles.shape
    count, slots = tile_cols.shape
    core = lax.axis_index("rep")
    here = lax.axis_index("row")
    half = rows * half_slots
    per_block = rows * slots
    mine = tiles.reshape(half, tile, tile)
    other = swap_cores(mine)

    lists = send_lists(tile_cols, rows)
    ranks = running(lists)
    totals = jnp.sum(lists.astype(jnp.int32), axis=2)
    slot = jnp.arange(per_block, dtype=jnp.int32)
    line, column = slot // slots, slot % slots
    loc = ((column // half_slots) ^ core) * half + line * half_slots + column % half_slots

    full = per_block // 2
    my_list = lax.dynamic_index_in_dim(lists, here, 0, False)
    my_rank = lax.dynamic_index_in_dim(ranks, here, 0, False)
    want = (jnp.arange(full, dtype=jnp.int32) * 2 + core)[None, :, None]
    match = my_list[:, None, :] & (my_rank[:, None, :] == want)
    index = jnp.sum(jnp.where(match, loc, 0), axis=2)

    starts, items = work_items(tile_cols, lists, ranks, rows, half_slots, here, core, loc)

    def run(caps):
        side_cap, next_cap, up3_cap, up_cap = caps

        def exchange(mine, other, index, starts, items):
            side, second, up3, up = gather_tiles(caps, (0, 1, 2, 2), index, mine, other)
            side = moved(side, {0: 1, 1: -1, 2: 1, 3: -1})
            up3 = moved(up3, {3: 4})
            second = moved(second, {0: 2, 1: 2, 2: -2, 3: -2})
            up = moved(up, {0: 4, 1: 4, 2: 4})
            side_next = moved(side, {0: 2, 1: 2})
            side_up = moved(side, {2: 4})
            up3_diag = moved(up3, {3: -3})
            next_up = moved(second, {0: 4, 1: 4})
            up_down = moved(up, {1: -1, 2: -1})
            counts = jnp.zeros((rows, tile), jnp.float32)
            counts = count_tiles((), rows, starts, items, counts, mine, other, [], 10**9)
            counts = count_tiles(
                (SIDE, NEXT, UP3, UP), rows, starts, items, counts, mine, other,
                [side, second, up3, up], 2 * 10**9,
            )
            return count_tiles(
                (SIDE_NEXT, SIDE_UP, NEXT_UP, UP3_DIAG, UP_DOWN), rows, starts, items, counts,
                mine, other, [side_next, side_up, next_up, up3_diag, up_down], 2 * 10**9,
            )

        return exchange

    brief = (full * 3 // 4, full * 5 // 8, full * 11 // 16, full * 15 // 32)
    place = jnp.arange(totals.shape[0]) % BACK
    bound = jnp.stack(
        [
            jnp.full_like(place, 2 * brief[0]),
            jnp.full_like(place, 2 * brief[1]),
            jnp.where(place == 3, 2 * brief[2], 2 * brief[3]),
        ],
        axis=1,
    )
    fits = jnp.all(totals <= bound)
    partial = lax.cond(fits, run(brief), run((full,) * 4), mine, other, index, starts, items)

    width = tile // 2
    keep = lax.dynamic_slice_in_dim(partial, core * width, width, 1)
    give = lax.dynamic_slice_in_dim(partial, (1 - core) * width, width, 1)
    return keep + swap_cores(give)


def solution(mesh):
    return jax.shard_map(
        body,
        mesh=mesh,
        in_specs=(P("row", "rep", None, None), P()),
        out_specs=P("row", "rep"),
        check_vma=False,
    )
```

time: 422 us -> 105 us (0.25)
  local copies, waits for them, and re-layouts: 138 us -> 2.69 us
  waiting for transfers between devices: 173 us -> 54.1 us
  matrix products: 75.9 us -> 1.7 us
  Pallas kernels: 0 us -> 21 us
  between operations: 13.4 us -> 0.97 us
  starting transfers between devices: 10.2 us -> 18 us
    ppermute x5 -> x11, waiting for transfers between devices: 165 us -> 54.1 us  [the longest x9 53.3 us: moved(): return lax.ppermute(x, 'row', [(i, j) for i, j in route if j < size])]
    dot_general x16 -> x6, matrix products: 75.9 us -> 1.7 us  [the longest x1 0.66 us: send_lists(): lax.dot_general(later, column, dims, preferred_element_type=jnp.float32)]
    gather x16 -> x0, local copies, waits for them, and re-layouts: 61.2 us -> none  [the longest x8 56.7 us: one_row(): panels = jnp.take(pool, local, axis=0)]
    dot_general x8 -> x0, local copies, waits for them, and re-layouts: 54.2 us -> none  [one_row(): jnp.einsum('kjp,pac->kjac', match.astype(jnp.bfloat16), whole_row, prefer...]
    pallas_call x0 -> x4, Pallas kernels: none -> 21 us  [the longest x3 15.5 us: count_tiles(): pl.pallas_call(lambda *refs: count_kernel(groups, rows, *refs), out_shape...]
    unnamed x9 -> x5, local copies, waits for them, and re-layouts: 13.9 us -> 0.8 us
    squeeze x8 -> x0, local copies, waits for them, and re-layouts: 8.62 us -> none  [body(): partial_counts = lax.map(one_row, (full, my_cols))]
    unnamed x2 -> x0, waiting for transfers between devices: 8.38 us -> none
  transfers between devices with their start and end apart: 6 -> 11, of which waited for: 5 -> 5; matrix products, arithmetic and copies ran while one was open for 3% -> 9% of each run, Pallas kernels for 0% -> 8%
where the time goes in v1:
time: 105 us
  waiting for transfers between devices  54.1 us (52%)
  Pallas kernels  21 us (20%)
  starting transfers between devices  18 us (17%)
  other arithmetic  5.89 us (6%)
  local copies, waits for them, and re-layouts  2.69 us (3%)
  matrix products  1.7 us (2%)
    ppermute x9, waiting for transfers between devices, moved(): return lax.ppermute(x, 'row', [(i, j) for i, j in route if j < size])  53.3 us
    pallas_call x3, Pallas kernels, count_tiles(): pl.pallas_call(lambda *refs: count_kernel(groups, rows, *refs), out_shape...  15.5 us
    ppermute x9, starting transfers between devices, moved(): return lax.ppermute(x, 'row', [(i, j) for i, j in route if j < size])  14.7 us
    pallas_call x1, Pallas kernels, gather_tiles(): pl.pallas_call(lambda *refs: gather_kernel(caps, lists, *refs), out_shape...  5.52 us
    ppermute x2, starting transfers between devices, swap_cores(): return lax.ppermute(x, 'rep', [(0, 1), (1, 0)])  3.39 us
  transfers between devices with their start and end apart: 11, of which 5 were waited for; matrix products, arithmetic and copies ran while one was open for 9% of the time, Pallas kernels for 8%

profile of v1, /device:TPU:25, one launch (start us, length us, event | category | flops | bytes accessed | tf_op | source)
XLA Modules:
  0.0 104.5 jit_solution(4481897758894540548)
XLA Ops:
  0.0 0.7 collective-permute-start.18
  0.7 0.8 copy.31
  9.4 1.2 %select_reduce_fusion = s32[1280]{0:T(1024)S(1)} fusion(s32[2048]{0:T(1024)S(1)} %sub.98, s32[2048]{0:T(1024)S(1)} %bitcast.37, s32[1280]{0:T(1024)S(1)} %iota_add_fusion), kind=kLoop, calls=%fused_computation | loop fusion | flops 7863040 | bytes 26624 | tf_op jit(solution)/shard_map/reduce_sum | solution.py:223
  10.6 89.7 %conditional.1 = (f32[8,128]{1,0:T(8,128)S(1)}) conditional(s32[]{:T(128)} %convert_element_type.49, (s32[11]{0:T(128)S(1)}, s32[1280]{0:T(1024)S(1)}, bf16[64,128,128]{2,1,0:T(8,128)(2,1)S(1)}, bf16[64,128,128]{2,1,0:T(8,128)(2,1)}, s32[3,64]{1,0:T(4,128)S(1)}) %tuple.25, (s32[11]{0:T(128)S(1)}, s32[1280]{0:T(1024)S(1)}, ...), branch_computations={%region_13.14_spmd, %region_14.15_spmd} | conditional | flops 5000999936 | bytes 116279160 | solution.py:290
  10.6 5.5 %branch_1_fun.5 = (bf16[48,128,128]{2,1,0:T(8,128)(2,1)}, bf16[40,128,128]{2,1,0:T(8,128)(2,1)}, bf16[44,128,128]{2,1,0:T(8,128)(2,1)}, bf16[30,128,128]{2,1,0:T(8,128)(2,1)}) custom-call(s32[3,64]{1,0:T(4,128)S(1)} %get-tuple-element.41.refs_0_, bf16[64,128,128]{2,1,0:T(8,128)(2,1)S(1)} %get-tuple-element.39.refs_3_.refs_1_, ...), custom_call_target="tpu_custom_call" | custom-call | flops 1000000 | bytes 10616832 | tf_op jit(solution)/shard_map/cond/branch_1_fun/pallas_call | solution.py:82
  16.1 1.3 %collective-permute-start.9 = (bf16[48,128,128]{2,1,0:T(8,128)(2,1)}, bf16[48,128,128]{2,1,0:T(8,128)(2,1)}, u32[]{:S(2)}, u32[]{:S(2)}) collective-permute-start(bf16[48,128,128]{2,1,0:T(8,128)(2,1)} %get-tuple-element.42), channel_id=1, source_target_pairs={{0,1},{1,0},{2,3},{3,2},{4,5},{5,4},{6,7},{7,6},{8,9},{9,8},{10,11... | collective-permute-start | bytes 4718600 | tf_op jit(solution)/shard_map/cond/branch_1_fun/ppermute | solution.py:27
  17.4 0.7 collective-permute-start.11
  18.2 1.3 %collective-permute-start.10 = (bf16[40,128,128]{2,1,0:T(8,128)(2,1)}, bf16[40,128,128]{2,1,0:T(8,128)(2,1)}, u32[]{:S(2)}, u32[]{:S(2)}) collective-permute-start(bf16[40,128,128]{2,1,0:T(8,128)(2,1)} %get-tuple-element.43), channel_id=1, source_target_pairs={{0,2},{1,3},{2,0},{3,1},{4,6},{5,7},{6,4},{7,5},{8,10},{9,11},{10,... | collective-permute-start | bytes 3932168 | tf_op jit(solution)/shard_map/cond/branch_1_fun/ppermute | solution.py:27
  19.5 1.3 %collective-permute-start.12 = (bf16[30,128,128]{2,1,0:T(8,128)(2,1)}, bf16[30,128,128]{2,1,0:T(8,128)(2,1)}, u32[]{:S(2)}, u32[]{:S(2)}) collective-permute-start(bf16[30,128,128]{2,1,0:T(8,128)(2,1)} %get-tuple-element.45), channel_id=1, source_target_pairs={{0,4},{1,5},{2,6},{4,8},{5,9},{6,10},{8,12},{9,13},{10,14},{16,20}... | collective-permute-start | bytes 2949128 | tf_op jit(solution)/shard_map/cond/branch_1_fun/ppermute | solution.py:27
  20.7 31.6 %collective-permute-done.9.refs_5_ = bf16[48,128,128]{2,1,0:T(8,128)(2,1)} collective-permute-done((bf16[48,128,128]{2,1,0:T(8,128)(2,1)}, bf16[48,128,128]{2,1,0:T(8,128)(2,1)}, u32[]{:S(2)}, u32[]{:S(2)}) %collective-permute-start.9) | collective-permute-done | bytes 1572896 | tf_op jit(solution)/shard_map/cond/branch_1_fun/ppermute | solution.py:27
  52.4 4.3 %collective-permute-start.13 = (bf16[48,128,128]{2,1,0:T(8,128)(2,1)}, bf16[48,128,128]{2,1,0:T(8,128)(2,1)}, u32[]{:S(2)}, u32[]{:S(2)}) collective-permute-start(bf16[48,128,128]{2,1,0:T(8,128)(2,1)} %collective-permute-done.9.refs_5_), channel_id=1, source_target_pairs={{0,2},{1,3},{4,6},{5,7},{8,10},{9,11},{12,14},{13,15},{16,18},{17,... | collective-permute-start | bytes 4718600 | tf_op jit(solution)/shard_map/cond/branch_1_fun/ppermute | solution.py:27
  56.7 1.9 %collective-permute-start.14 = (bf16[48,128,128]{2,1,0:T(8,128)(2,1)}, bf16[48,128,128]{2,1,0:T(8,128)(2,1)}, u32[]{:S(2)}, u32[]{:S(2)}) collective-permute-start(bf16[48,128,128]{2,1,0:T(8,128)(2,1)} %collective-permute-done.9.refs_5_), channel_id=1, source_target_pairs={{2,6},{6,10},{10,14},{18,22},{22,26},{26,30}} | collective-permute-start | bytes 4718600 | tf_op jit(solution)/shard_map/cond/branch_1_fun/ppermute | solution.py:27
  58.6 1.3 %collective-permute-start.16 = (bf16[44,128,128]{2,1,0:T(8,128)(2,1)S(1)}, bf16[44,128,128]{2,1,0:T(8,128)(2,1)}, u32[]{:S(2)}, u32[]{:S(2)}) collective-permute-start(bf16[44,128,128]{2,1,0:T(8,128)(2,1)S(1)} %collective-permute-done.11.refs_7_), channel_id=1, source_target_pairs={{3,0},{7,4},{11,8},{15,12},{19,16},{23,20},{27,24},{31,28}} | collective-permute-start | bytes 4325384 | tf_op jit(solution)/shard_map/cond/branch_1_fun/ppermute | solution.py:27
  59.9 1.3 %collective-permute-start.15 = (bf16[40,128,128]{2,1,0:T(8,128)(2,1)}, bf16[40,128,128]{2,1,0:T(8,128)(2,1)}, u32[]{:S(2)}, u32[]{:S(2)}) collective-permute-start(bf16[40,128,128]{2,1,0:T(8,128)(2,1)} %collective-permute-done.10.refs_6_), channel_id=1, source_target_pairs={{0,4},{1,5},{4,8},{5,9},{8,12},{9,13},{16,20},{17,21},{20,24},{21,... | collective-permute-start | bytes 3932168 | tf_op jit(solution)/shard_map/cond/branch_1_fun/ppermute | solution.py:27
  61.2 1.3 %collective-permute-start.17 = (bf16[30,128,128]{2,1,0:T(8,128)(2,1)}, bf16[30,128,128]{2,1,0:T(8,128)(2,1)}, u32[]{:S(2)}, u32[]{:S(2)}) collective-permute-start(bf16[30,128,128]{2,1,0:T(8,128)(2,1)} %collective-permute-done.12.refs_8_), channel_id=1, source_target_pairs={{1,0},{2,1},{5,4},{6,5},{9,8},{10,9},{13,12},{14,13},{17,16},{18,1... | collective-permute-start | bytes 2949128 | tf_op jit(solution)/shard_map/cond/branch_1_fun/ppermute | solution.py:27
  63.1 4.6 %branch_1_fun.4.refs_2_ = f32[8,128]{1,0:T(8,128)} custom-call(s32[11]{0:T(128)S(1)} %get-tuple-element.37.refs_0_, s32[1280]{0:T(1024)S(1)} %get-tuple-element.38.refs_1_, f32[8,128]{1,0:T(8,128)} %broadcast_33_refs_2_.0.refs_2_, bf16[64,128,128]{2,1,0:T(8,128)(2,1)S(1)} %get-tuple-element.39.refs_3_.refs_1_, ...), custom_call_target="tpu_custom_call" | custom-call | flops 1000000000 | bytes 8000000 | tf_op jit(solution)/shard_map/cond/branch_1_fun/pallas_call | solution.py:148
  67.7 4.0 %branch_1_fun.6.refs_2_ = f32[8,128]{1,0:T(8,128)} custom-call(s32[11]{0:T(128)S(1)} %get-tuple-element.37.refs_0_, s32[1280]{0:T(1024)S(1)} %get-tuple-element.38.refs_1_, f32[8,128]{1,0:T(8,128)} %branch_1_fun.4.refs_2_, bf16[64,128,128]{2,1,0:T(8,128)(2,1)S(1)} %get-tuple-element.39.refs_3_.refs_1_, ...), custom_call_target="tpu_custom_call" | custom-call | flops 2000000000 | bytes 8000000 | tf_op jit(solution)/shard_map/cond/branch_1_fun/pallas_call | solution.py:148
  71.7 14.2 %collective-permute-done.17.refs_9_ = bf16[30,128,128]{2,1,0:T(8,128)(2,1)} collective-permute-done((bf16[30,128,128]{2,1,0:T(8,128)(2,1)}, bf16[30,128,128]{2,1,0:T(8,128)(2,1)}, u32[]{:S(2)}, u32[]{:S(2)}) %collective-permute-start.17) | collective-permute-done | bytes 983072 | tf_op jit(solution)/shard_map/cond/branch_1_fun/ppermute | solution.py:27
  85.9 5.3 %collective-permute-done.15.refs_7_ = bf16[40,128,128]{2,1,0:T(8,128)(2,1)} collective-permute-done((bf16[40,128,128]{2,1,0:T(8,128)(2,1)}, bf16[40,128,128]{2,1,0:T(8,128)(2,1)}, u32[]{:S(2)}, u32[]{:S(2)}) %collective-permute-start.15) | collective-permute-done | bytes 1310752 | tf_op jit(solution)/shard_map/cond/branch_1_fun/ppermute | solution.py:27
  91.2 2.2 %collective-permute-done.16.refs_8_ = bf16[44,128,128]{2,1,0:T(8,128)(2,1)} collective-permute-done((bf16[44,128,128]{2,1,0:T(8,128)(2,1)S(1)}, bf16[44,128,128]{2,1,0:T(8,128)(2,1)}, u32[]{:S(2)}, u32[]{:S(2)}) %collective-permute-start.16) | collective-permute-done | bytes 1441824 | tf_op jit(solution)/shard_map/cond/branch_1_fun/ppermute | solution.py:27
  93.4 6.8 %branch_1_fun.7 = f32[8,128]{1,0:T(8,128)S(1)} custom-call(s32[11]{0:T(128)S(1)} %get-tuple-element.37.refs_0_, s32[1280]{0:T(1024)S(1)} %get-tuple-element.38.refs_1_, f32[8,128]{1,0:T(8,128)} %branch_1_fun.6.refs_2_, bf16[64,128,128]{2,1,0:T(8,128)(2,1)S(1)} %get-tuple-element.39.refs_3_.refs_1_, bf16[64,128,128]{2,1,0:T(8,128)(2,1)} %get-tuple-element.40.refs_4_.refs_2_, ...), custom_call_target="tpu_custom_call" | custom-call | flops 2000000000 | bytes 8000000 | tf_op jit(solution)/shard_map/cond/branch_1_fun/pallas_call | solution.py:148
  100.3 2.7 %collective-permute-start.19 = (f32[8,64]{1,0:T(8,128)S(1)}, f32[8,64]{1,0:T(8,128)S(1)}, u32[]{:S(2)}, u32[]{:S(2)}) collective-permute-start(f32[8,64]{1,0:T(8,128)S(1)} %constant_dynamic-slice_fusion.1), channel_id=1, source_target_pairs={{0,16},{16,0},{1,17},{17,1},{2,18},{18,2},{3,19},{19,3},{4,20},{20... | collective-permute-start | bytes 6152 | tf_op jit(solution)/shard_map/ppermute | solution.py:21
  103.0 0.8 collective-permute-done.19
  103.9 0.7 dynamic-slice_add_fusion
  (77 shorter events, 7.7 us)
Async XLA Ops:
  0.0 4.5 %copy-start.2 = (s32[128,16]{0,1:T(8,128)S(1)}, s32[128,16]{0,1:T(8,128)}, u32[]{:S(2)}) copy-start(s32[128,16]{0,1:T(8,128)} %param.5) | copy-start | bytes 24580
  0.0 10.6 %collective-permute-start.18 = (bf16[64,128,128]{2,1,0:T(8,128)(2,1)}, bf16[64,128,128]{2,1,0:T(8,128)(2,1)}, u32[]{:S(2)}, u32[]{:S(2)}) collective-permute-start(bf16[64,128,128]{2,1,0:T(8,128)(2,1)} %bitcast.31), channel_id=1, source_target_pairs={{0,16},{16,0},{1,17},{17,1},{2,18},{18,2},{3,19},{19,3},{4,20},{20... | collective-permute-start | bytes 6291464 | tf_op jit(solution)/shard_map/ppermute | solution.py:21
  2.2 8.4 %copy-start = (bf16[8,8,128,128]{3,2,1,0:T(8,128)(2,1)S(1)}, bf16[8,8,128,128]{3,2,1,0:T(8,128)(2,1)}, u32[]{:S(2)}) copy-start(bf16[8,8,128,128]{3,2,1,0:T(8,128)(2,1)} %param.4) | copy-start | bytes 6291460
  16.1 36.3 %collective-permute-start.9 = (bf16[48,128,128]{2,1,0:T(8,128)(2,1)}, bf16[48,128,128]{2,1,0:T(8,128)(2,1)}, u32[]{:S(2)}, u32[]{:S(2)}) collective-permute-start(bf16[48,128,128]{2,1,0:T(8,128)(2,1)} %get-tuple-element.42), channel_id=1, source_target_pairs={{0,1},{1,0},{2,3},{3,2},{4,5},{5,4},{6,7},{7,6},{8,9},{9,8},{10,11... | collective-permute-start | bytes 4718600 | tf_op jit(solution)/shard_map/cond/branch_1_fun/ppermute | solution.py:27
  17.4 41.2 %collective-permute-start.11 = (bf16[44,128,128]{2,1,0:T(8,128)(2,1)}, bf16[44,128,128]{2,1,0:T(8,128)(2,1)S(1)}, u32[]{:S(2)}, u32[]{:S(2)}) collective-permute-start(bf16[44,128,128]{2,1,0:T(8,128)(2,1)} %get-tuple-element.44), channel_id=1, source_target_pairs={{3,7},{7,11},{11,15},{19,23},{23,27},{27,31}} | collective-permute-start | bytes 4325384 | tf_op jit(solution)/shard_map/cond/branch_1_fun/ppermute | solution.py:27
  18.2 41.7 %collective-permute-start.10 = (bf16[40,128,128]{2,1,0:T(8,128)(2,1)}, bf16[40,128,128]{2,1,0:T(8,128)(2,1)}, u32[]{:S(2)}, u32[]{:S(2)}) collective-permute-start(bf16[40,128,128]{2,1,0:T(8,128)(2,1)} %get-tuple-element.43), channel_id=1, source_target_pairs={{0,2},{1,3},{2,0},{3,1},{4,6},{5,7},{6,4},{7,5},{8,10},{9,11},{10,... | collective-permute-start | bytes 3932168 | tf_op jit(solution)/shard_map/cond/branch_1_fun/ppermute | solution.py:27
  19.5 41.7 %collective-permute-start.12 = (bf16[30,128,128]{2,1,0:T(8,128)(2,1)}, bf16[30,128,128]{2,1,0:T(8,128)(2,1)}, u32[]{:S(2)}, u32[]{:S(2)}) collective-permute-start(bf16[30,128,128]{2,1,0:T(8,128)(2,1)} %get-tuple-element.45), channel_id=1, source_target_pairs={{0,4},{1,5},{2,6},{4,8},{5,9},{6,10},{8,12},{9,13},{10,14},{16,20}... | collective-permute-start | bytes 2949128 | tf_op jit(solution)/shard_map/cond/branch_1_fun/ppermute | solution.py:27
  52.4 41.0 %collective-permute-start.13 = (bf16[48,128,128]{2,1,0:T(8,128)(2,1)}, bf16[48,128,128]{2,1,0:T(8,128)(2,1)}, u32[]{:S(2)}, u32[]{:S(2)}) collective-permute-start(bf16[48,128,128]{2,1,0:T(8,128)(2,1)} %collective-permute-done.9.refs_5_), channel_id=1, source_target_pairs={{0,2},{1,3},{4,6},{5,7},{8,10},{9,11},{12,14},{13,15},{16,18},{17,... | collective-permute-start | bytes 4718600 | tf_op jit(solution)/shard_map/cond/branch_1_fun/ppermute | solution.py:27
  56.7 36.7 %collective-permute-start.14 = (bf16[48,128,128]{2,1,0:T(8,128)(2,1)}, bf16[48,128,128]{2,1,0:T(8,128)(2,1)}, u32[]{:S(2)}, u32[]{:S(2)}) collective-permute-start(bf16[48,128,128]{2,1,0:T(8,128)(2,1)} %collective-permute-done.9.refs_5_), channel_id=1, source_target_pairs={{2,6},{6,10},{10,14},{18,22},{22,26},{26,30}} | collective-permute-start | bytes 4718600 | tf_op jit(solution)/shard_map/cond/branch_1_fun/ppermute | solution.py:27
  58.6 9.2 %copy-start.1 = (bf16[44,128,128]{2,1,0:T(8,128)(2,1)}, bf16[44,128,128]{2,1,0:T(8,128)(2,1)S(1)}, u32[]{:S(2)}) copy-start(bf16[44,128,128]{2,1,0:T(8,128)(2,1)S(1)} %collective-permute-done.11.refs_7_) | copy-start | bytes 4325380 | tf_op jit(solution)/shard_map/cond
  58.6 34.8 %collective-permute-start.16 = (bf16[44,128,128]{2,1,0:T(8,128)(2,1)S(1)}, bf16[44,128,128]{2,1,0:T(8,128)(2,1)}, u32[]{:S(2)}, u32[]{:S(2)}) collective-permute-start(bf16[44,128,128]{2,1,0:T(8,128)(2,1)S(1)} %collective-permute-done.11.refs_7_), channel_id=1, source_target_pairs={{3,0},{7,4},{11,8},{15,12},{19,16},{23,20},{27,24},{31,28}} | collective-permute-start | bytes 4325384 | tf_op jit(solution)/shard_map/cond/branch_1_fun/ppermute | solution.py:27
  59.9 31.3 %collective-permute-start.15 = (bf16[40,128,128]{2,1,0:T(8,128)(2,1)}, bf16[40,128,128]{2,1,0:T(8,128)(2,1)}, u32[]{:S(2)}, u32[]{:S(2)}) collective-permute-start(bf16[40,128,128]{2,1,0:T(8,128)(2,1)} %collective-permute-done.10.refs_6_), channel_id=1, source_target_pairs={{0,4},{1,5},{4,8},{5,9},{8,12},{9,13},{16,20},{17,21},{20,24},{21,... | collective-permute-start | bytes 3932168 | tf_op jit(solution)/shard_map/cond/branch_1_fun/ppermute | solution.py:27
  61.2 24.7 %collective-permute-start.17 = (bf16[30,128,128]{2,1,0:T(8,128)(2,1)}, bf16[30,128,128]{2,1,0:T(8,128)(2,1)}, u32[]{:S(2)}, u32[]{:S(2)}) collective-permute-start(bf16[30,128,128]{2,1,0:T(8,128)(2,1)} %collective-permute-done.12.refs_8_), channel_id=1, source_target_pairs={{1,0},{2,1},{5,4},{6,5},{9,8},{10,9},{13,12},{14,13},{17,16},{18,1... | collective-permute-start | bytes 2949128 | tf_op jit(solution)/shard_map/cond/branch_1_fun/ppermute | solution.py:27
  100.3 3.5 %collective-permute-start.19 = (f32[8,64]{1,0:T(8,128)S(1)}, f32[8,64]{1,0:T(8,128)S(1)}, u32[]{:S(2)}, u32[]{:S(2)}) collective-permute-start(f32[8,64]{1,0:T(8,128)S(1)} %constant_dynamic-slice_fusion.1), channel_id=1, source_target_pairs={{0,16},{16,0},{1,17},{17,1},{2,18},{18,2},{3,19},{19,3},{4,20},{20... | collective-permute-start | bytes 6152 | tf_op jit(solution)/shard_map/ppermute | solution.py:21
